TPU v7x, 256 devices: a whole 4x4x8 slice. The times are simulated.
256 devices in a mesh: ep: 64 (over z, y, core), fsdp: 4 (over x).
Axes of the slice: x: 4, y: 4, z: 8, core: 2. Of those that a mesh axis runs over, the one named last changes fastest.
Arguments:
- train_gate: float32 [64, 2048, 1024], P('ep', 'fsdp'), may hold values from -0.1875 to 0.1875
- other_gate: float32 [64, 2048, 1024], P('ep', 'fsdp'), may hold values from -0.125 to 0.125
- train_up: float32 [64, 2048, 1024], P('ep', 'fsdp'), may hold values from -0.1875 to 0.1875
- other_up: float32 [64, 2048, 1024], P('ep', 'fsdp'), may hold values from -0.125 to 0.125
- mix_share: float32 [64], P('ep'), may hold values from 0.2 to 0.8
- router_weight: float32 [2048, 64], P('fsdp', 'ep'), may hold values from -0.125 to 0.125
- router_gain: float32 [2048], P('fsdp'), may hold values from 0.25 to 1.75
Outputs:
- ready_gate: bfloat16 [64, 2048, 1024], P('ep')
- ready_up: bfloat16 [64, 2048, 1024], P('ep')
- scale_gate: float32 [64, 1024], P('ep')
- scale_up: float32 [64, 1024], P('ep')
- serve_router: bfloat16 [2048, 64], replicated
All inputs are finite; a program needn't handle non-finite values. Where the computation divides by a largest or mean magnitude, that divisor is 1e-20 or more.
Results may differ from a plain program's by a relative error of at most 0.001.
Values may be sent and summed in bfloat16 or wider, within the bound.
A program may use at most 64 MiB of HBM per device.

v0:
```python
import jax
import jax.numpy as jnp
from jax import lax
from jax.sharding import PartitionSpec as P


def sent_to_all(array, axis):
    length = lax.axis_size(axis)
    return lax.all_to_all(
        jnp.broadcast_to(array[None], (length, *array.shape)), axis, 0, 0, tiled=True
    )


def of_everyone(array, axis):
    everything = sent_to_all(array, axis)
    return jnp.max(everything, axis=0)


def together(arrays, axis):
    ends = [0]
    for a in arrays:
        ends.append(ends[-1] + a.size)
    subtotal = of_everyone(jnp.concatenate([a.ravel() for a in arrays]), axis)
    return tuple((subtotal[b:e].reshape(a.shape) for a, b, e in zip(arrays, ends, ends[1:])))


def side_by_side(arrays, axis, dim, along):
    widths = [a.shape[along] for a in arrays]
    both = jnp.concatenate(arrays, axis=along)
    out = lax.all_gather(both, axis, axis=dim, tiled=True)
    return tuple(jnp.split(out, [sum(widths[:k]) for k in range(1, len(widths))], axis=along))


def joined_along(pieces, dim):
    pieces = jnp.moveaxis(pieces, 0, dim)
    dims = pieces.shape
    return pieces.reshape(*dims[:dim], dims[dim] * dims[dim + 1], *dims[dim + 2 :])


def gathered_copies(array, axis, dim):
    pieces = sent_to_all(array, axis)
    return joined_along(pieces, dim)


def per_device(train_gate, other_gate, train_up, other_up, mix_share, router_weight, router_gain):
    latest_gate = (
        mix_share[:, None, None] * train_gate + (1.0 - mix_share[:, None, None]) * other_gate
    )
    latest_up = mix_share[:, None, None] * train_up + (1.0 - mix_share[:, None, None]) * other_up
    scale_gate, scale_up = together(
        (jnp.max(jnp.abs(latest_gate), axis=1), jnp.max(jnp.abs(latest_up), axis=1)), "fsdp"
    )
    narrow_gate, narrow_up = (
        (latest_gate / jnp.expand_dims(scale_gate, 1)).astype(jnp.bfloat16),
        (latest_up / jnp.expand_dims(scale_up, 1)).astype(jnp.bfloat16),
    )
    ready_gate, ready_up = side_by_side((narrow_gate, narrow_up), "fsdp", 1, 0)
    part_router = (router_weight * router_gain[:, None]).astype(jnp.bfloat16)
    row_router = lax.all_gather(part_router, "fsdp", axis=0, tiled=True)
    serve_router = gathered_copies(row_router, "ep", 1)
    return (ready_gate, ready_up, scale_gate, scale_up, serve_router)


def solution(mesh):
    placed = (
        P("ep", "fsdp", None),
        P("ep", "fsdp", None),
        P("ep", "fsdp", None),
        P("ep", "fsdp", None),
        P("ep"),
        P("fsdp", "ep"),
        P("fsdp"),
    )
    return jax.shard_map(
        per_device,
        mesh=mesh,
        in_specs=placed,
        out_specs=(P("ep", None, None), P("ep", None, None), P("ep", None), P("ep", None), P()),
        check_vma=False,
    )
```

profile of v0, /device:TPU:1, one launch (start us, length us, event | category | flops | bytes accessed | tf_op | source)
XLA Modules:
  0.0 127.2 jit_solution(10108246183193982940)
XLA Ops:
  7.2 0.0 all-gather.2.cloned.1.call-start
  7.9 0.0 copy-start.1
  7.9 2.6 %abs_reduce_fusion.1 = f32[1024]{0:T(1024)S(1)} fusion(f32[1,512,1024]{2,1,0:T(8,128)} %param.8, f32[]{:T(128)} %bitcast.1, f32[1,512,1024]{2,1,0:T(8,128)} %param.7, f32[]{:T(128)} %bitcast.13), kind=kLoop, calls=%fused_computation.5 | loop fusion | flops 2620416 | bytes 4198408 | tf_op jit(solution)/shard_map/reduce_max | solution.py:51
  10.5 0.2 copy-done
  10.7 0.6 copy-done.1
  11.3 0.3 abs_reduce_fusion
  11.7 8.9 %all_to_all.11 = f32[4,1,2048]{2,1,0:T(1,128)S(1)} all-to-all(f32[4,1,2048]{2,1,0:T(1,128)S(1)} %broadcast_in_dim.8), channel_id=1, replica_groups=mesh['ep'=64,'fsdp'=4] {'fsdp'}, dimensions={0} | all-to-all | bytes 65536 | tf_op jit(solution)/shard_map/all_to_all | solution.py:9
  20.7 0.0 copy-start.2
  20.7 0.0 copy-start.3
  20.7 4.0 %divide_convert_fusion = (bf16[1,512,1024]{2,1,0:T(8,128)(2,1)S(1)}, bf16[1,512,1024]{2,1,0:T(8,128)(2,1)S(1)}) fusion(f32[1024]{0:T(1024)S(1)} %get-tuple-element.8, f32[1,512,1024]{2,1,0:T(8,128)S(1)} %copy-done, f32[]{:T(128)} %bitcast.1, f32[1,512,1024]{2,1,0:T(8,128)} %param.9, f32[]{:T(128)} %bitcast.15, f32[1024]{0:T(1024)S(1)} %get-tuple-element.7, ...), kind=kLoop, calls=%fused_computation.1 | loop fusion | flops 5242880 | bytes 10493960 | tf_op jit(solution)/shard_map/convert_element_type | solution.py:55
  24.7 1.5 %pad_maximum_fusion = bf16[2,512,1024]{2,1,0:T(8,128)(2,1)} fusion(bf16[1,512,1024]{2,1,0:T(8,128)(2,1)S(1)} %get-tuple-element.9, bf16[1,512,1024]{2,1,0:T(8,128)(2,1)S(1)} %get-tuple-element.10), kind=kLoop, calls=%fused_computation | loop fusion | flops 1048576 | bytes 4194304 | tf_op jit(solution)/shard_map/concatenate | solution.py:29
  26.2 0.0 all-gather.2.cloned.1.call-update
  26.2 0.7 copy-done.4
  26.9 0.0 copy-done.5
  26.9 8.1 %all_gather.7 = bf16[2048,1]{0,1:T(2,128)(2,1)S(1)} all-gather(bf16[512,1]{0,1:T(2,128)(2,1)S(1)} %multiply_convert_fusion), channel_id=1, replica_groups=mesh['ep'=64,'fsdp'=4] {'fsdp'}, dimensions={0}, use_global_device_ids=true | all-gather | bytes 5120 | tf_op jit(solution)/shard_map/all_gather | solution.py:59
  35.0 0.3 broadcast_bitcast_fusion
  35.3 0.5 broadcast.11
  35.8 2.2 %reduce.4 = bf16[64,2048]{1,0:T(8,128)(2,1)S(1)} reduce(bf16[64,1,2048]{2,1,0:T(2,128)(2,1)S(1)} %broadcast_bitcast_fusion, bf16[]{:T(256)} %broadcast.11), dimensions={1}, to_apply=%broadcast_bitcast_fusion.reduce_sub_computation | reduce | bytes 524290
  38.0 0.2 reshape.52
  38.2 28.9 %all_to_all.12 = bf16[64,2,1024]{2,1,0:T(2,128)(2,1)S(1)} all-to-all(bf16[64,2,1024]{2,1,0:T(2,128)(2,1)S(1)} %reshape.52), channel_id=1, replica_groups=mesh['ep'=64,'fsdp'=4] {'ep'}, dimensions={0} | all-to-all | bytes 524288 | tf_op jit(solution)/shard_map/all_to_all | solution.py:9
  67.1 0.2 reshape.53
  67.3 0.9 copy.20
  68.2 46.1 %all-gather.2.cloned.1.call-done = bf16[2,2048,1024]{2,1,0:T(8,128)(2,1)} async-done(((bf16[2,512,1024]{2,1,0:T(8,128)(2,1)}), bf16[2,2048,1024]{2,1,0:T(8,128)(2,1)}) %all-gather.2.cloned.1.call-update) | async-done | bytes 8388624 | tf_op jit(solution)/shard_map/all_gather | solution.py:30
  114.3 6.0 %fusion = (bf16[1,2048,1024]{2,1,0:T(8,128)(2,1)}, bf16[1,2048,1024]{2,1,0:T(8,128)(2,1)}) fusion(bf16[2,2048,1024]{2,1,0:T(8,128)(2,1)} %all-gather.2.cloned.1.call-done), kind=kLoop, calls=%fused_computation.10 | loop fusion | bytes 16777216 | tf_op jit(solution)/shard_map/split | solution.py:31
  (11 shorter events, 0.1 us)
Async XLA Ops:
  7.2 107.2 %all-gather.2.cloned.1.call-start = ((), (), s32[]{:S(2)}) async-start(), calls=%async_computation.2 | async-start | bytes 10485760 | tf_op jit(solution)/shard_map/all_gather | solution.py:30
  7.9 2.9 %copy-start = (f32[1,512,1024]{2,1,0:T(8,128)S(1)}, f32[1,512,1024]{2,1,0:T(8,128)}, u32[]{:S(2)}) copy-start(f32[1,512,1024]{2,1,0:T(8,128)} %param.10) | copy-start | bytes 6291460
  7.9 3.5 %copy-start.1 = (f32[1,512,1024]{2,1,0:T(8,128)S(1)}, f32[1,512,1024]{2,1,0:T(8,128)}, u32[]{:S(2)}) copy-start(f32[1,512,1024]{2,1,0:T(8,128)} %param.9) | copy-start | bytes 6291460
  20.7 4.0 %copy-start.2 = (f32[1024]{0:T(1024)}, f32[1024]{0:T(1024)S(1)}, u32[]{:S(2)}) copy-start(f32[1024]{0:T(1024)S(1)} %get-tuple-element.7) | copy-start | bytes 12292
  20.7 4.0 %copy-start.3 = (f32[1024]{0:T(1024)}, f32[1024]{0:T(1024)S(1)}, u32[]{:S(2)}) copy-start(f32[1024]{0:T(1024)S(1)} %get-tuple-element.8) | copy-start | bytes 12292
  26.2 0.7 copy-start.4
  26.2 0.7 copy-start.5
Sparse Core Ops, SparseCore 0:
  26.3 87.9 all-gather.1
where the time goes:
time: 127 us
  waiting for transfers between devices  46.1 us (36%)
  blocking collectives  46 us (36%)
  between operations  14.8 us (12%)
  other arithmetic  10.6 us (8%)
  local copies, waits for them, and re-layouts  9.61 us (8%)
    all_gather x1, waiting for transfers between devices, side_by_side(): out = lax.all_gather(both, axis, axis=dim, tiled=True)  46.1 us
    all_to_all x2, blocking collectives, sent_to_all(): lax.all_to_all(jnp.broadcast_to(array[None], (length, *array.shape)), axi...  37.9 us
    all_gather x1, blocking collectives, per_device(): row_router = lax.all_gather(part_router, 'fsdp', axis=0, tiled=True)  8.13 us
    split x1, local copies, waits for them, and re-layouts, side_by_side(): jnp.split(out, [sum(widths[:k]) for k in range(1, len(widths))], axis=along)  6.02 us
    convert_element_type x1, other arithmetic, per_device(): (latest_up / jnp.expand_dims(scale_up, 1)).astype(jnp.bfloat16)  3.95 us
    unnamed x16, local copies, waits for them, and re-layouts  2.71 us
    reduce_max x1, other arithmetic, per_device(): jnp.max(jnp.abs(latest_gate), axis=1)  2.63 us
  transfers between devices with their start and end apart: 1, of which 1 were waited for; matrix products, arithmetic and copies ran while one was open for 3% of the time, Pallas kernels for 0%

commit v1 on v0

--- a/solution.py
+++ b/solution.py
@@ -2,6 +2,14 @@
 import jax.numpy as jnp
 from jax import lax
 from jax.sharding import PartitionSpec as P
+
+
+def gather_by_exchange(value, axis, dim):
+    devices = lax.axis_size(axis)
+    repeats = [devices if d == dim else 1 for d in range(value.ndim)]
+    return lax.all_to_all(
+        jnp.tile(value, repeats), axis, split_axis=dim, concat_axis=dim, tiled=True
+    )
 
 
 def sent_to_all(array, axis):
@@ -56,7 +64,7 @@
     )
     ready_gate, ready_up = side_by_side((narrow_gate, narrow_up), "fsdp", 1, 0)
     part_router = (router_weight * router_gain[:, None]).astype(jnp.bfloat16)
-    row_router = lax.all_gather(part_router, "fsdp", axis=0, tiled=True)
+    row_router = gather_by_exchange(part_router, "fsdp", 0)
     serve_router = gathered_copies(row_router, "ep", 1)
     return (ready_gate, ready_up, scale_gate, scale_up, serve_router)
 

time: 127 us -> 127 us (level)
  blocking collectives: 46 us -> 43.2 us
  waiting for transfers between devices: 46.1 us -> 48.2 us
    all_gather x1 -> x0, blocking collectives: 8.13 us -> none  [per_device(): row_router = lax.all_gather(part_router, 'fsdp', axis=0, tiled=True)]
    all_to_all x0 -> x1, blocking collectives: none -> 6.48 us  [gather_by_exchange(): lax.all_to_all(jnp.tile(value, repeats), axis, split_axis=dim, concat_axi...]
    all_gather x1, waiting for transfers between devices: 46.1 us -> 48.2 us  [side_by_side(): out = lax.all_gather(both, axis, axis=dim, tiled=True)]
    unnamed x1 -> x2, other arithmetic: 2.15 us -> 2.83 us
    unnamed x16 -> x20, local copies, waits for them, and re-layouts: 2.71 us -> 2.75 us
  transfers between devices with their start and end apart: 1 -> 1, of which waited for: 1 -> 1; matrix products, arithmetic and copies ran while one was open for 3% -> 4% of each run, Pallas kernels for 0% -> 0%
where the time goes in v1:
time: 127 us
  waiting for transfers between devices  48.2 us (38%)
  blocking collectives  43.2 us (34%)
  between operations  14.8 us (12%)
  other arithmetic  11.3 us (9%)
  local copies, waits for them, and re-layouts  9.68 us (8%)
    all_gather x1, waiting for transfers between devices, side_by_side(): out = lax.all_gather(both, axis, axis=dim, tiled=True)  48.2 us
    all_to_all x2, blocking collectives, sent_to_all(): lax.all_to_all(jnp.broadcast_to(array[None], (length, *array.shape)), axi...  36.7 us
    all_to_all x1, blocking collectives, gather_by_exchange(): lax.all_to_all(jnp.tile(value, repeats), axis, split_axis=dim, concat_axi...  6.48 us
    split x1, local copies, waits for them, and re-layouts, side_by_side(): jnp.split(out, [sum(widths[:k]) for k in range(1, len(widths))], axis=along)  6.02 us
    convert_element_type x1, other arithmetic, per_device(): (latest_up / jnp.expand_dims(scale_up, 1)).astype(jnp.bfloat16)  3.95 us
    unnamed x2, other arithmetic  2.83 us
    unnamed x20, local copies, waits for them, and re-layouts  2.75 us
    reduce_max x1, other arithmetic, per_device(): jnp.max(jnp.abs(latest_gate), axis=1)  2.63 us
  transfers between devices with their start and end apart: 1, of which 1 were waited for; matrix products, arithmetic and copies ran while one was open for 4% of the time, Pallas kernels for 0%

profile of v1, /device:TPU:1, one launch (start us, length us, event | category | flops | bytes accessed | tf_op | source)
XLA Modules:
  0.0 127.2 jit_solution(5256462546767895766)
XLA Ops:
  7.2 0.0 all-gather.2.cloned.1.call-start
  7.9 2.6 %abs_reduce_fusion.1 = f32[1024]{0:T(1024)S(1)} fusion(f32[1,512,1024]{2,1,0:T(8,128)} %param.8, f32[]{:T(128)} %bitcast.1, f32[1,512,1024]{2,1,0:T(8,128)} %param.7, f32[]{:T(128)} %bitcast.19), kind=kLoop, calls=%fused_computation.5 | loop fusion | flops 2620416 | bytes 4198408 | tf_op jit(solution)/shard_map/reduce_max | solution.py:59
  10.5 0.2 copy-done
  10.7 0.6 copy-done.1
  11.3 0.3 abs_reduce_fusion
  11.7 8.9 %all_to_all.17 = f32[4,1,2048]{2,1,0:T(1,128)S(1)} all-to-all(f32[4,1,2048]{2,1,0:T(1,128)S(1)} %broadcast_in_dim.8), channel_id=1, replica_groups=mesh['ep'=64,'fsdp'=4] {'fsdp'}, dimensions={0} | all-to-all | bytes 65536 | tf_op jit(solution)/shard_map/all_to_all | solution.py:17
  20.7 0.0 copy-start.2
  20.7 0.0 copy-start.3
  20.7 4.0 %divide_convert_fusion = (bf16[1,512,1024]{2,1,0:T(8,128)(2,1)S(1)}, bf16[1,512,1024]{2,1,0:T(8,128)(2,1)S(1)}) fusion(f32[1024]{0:T(1024)S(1)} %get-tuple-element.8, f32[1,512,1024]{2,1,0:T(8,128)S(1)} %copy-done, f32[]{:T(128)} %bitcast.1, f32[1,512,1024]{2,1,0:T(8,128)} %param.9, f32[]{:T(128)} %bitcast.21, f32[1024]{0:T(1024)S(1)} %get-tuple-element.7, ...), kind=kLoop, calls=%fused_computation.1 | loop fusion | flops 5242880 | bytes 10493960 | tf_op jit(solution)/shard_map/convert_element_type | solution.py:63
  24.7 1.5 %pad_maximum_fusion = bf16[2,512,1024]{2,1,0:T(8,128)(2,1)} fusion(bf16[1,512,1024]{2,1,0:T(8,128)(2,1)S(1)} %get-tuple-element.9, bf16[1,512,1024]{2,1,0:T(8,128)(2,1)S(1)} %get-tuple-element.10), kind=kLoop, calls=%fused_computation | loop fusion | flops 1048576 | bytes 4194304 | tf_op jit(solution)/shard_map/concatenate | solution.py:37
  26.2 0.0 all-gather.2.cloned.1.call-update
  26.2 0.7 copy-done.4
  26.9 0.0 copy-done.5
  26.9 0.5 broadcast.16
  27.4 0.7 reduce.7
  28.1 6.5 %all_to_all.18 = bf16[4,2,256]{2,1,0:T(2,128)(2,1)S(1)} all-to-all(bf16[4,2,256]{2,1,0:T(2,128)(2,1)S(1)} %reshape.62), channel_id=1, replica_groups=mesh['ep'=64,'fsdp'=4] {'fsdp'}, dimensions={0} | all-to-all | bytes 8192 | tf_op jit(solution)/shard_map/all_to_all | solution.py:10
  34.7 0.3 broadcast_bitcast_fusion
  34.9 2.2 %reduce.8 = bf16[64,2048]{1,0:T(8,128)(2,1)S(1)} reduce(bf16[64,1,2048]{2,1,0:T(2,128)(2,1)S(1)} %broadcast_bitcast_fusion, bf16[]{:T(256)} %broadcast.16), dimensions={1}, to_apply=%broadcast_bitcast_fusion.reduce_sub_computation | reduce | bytes 524290
  37.1 0.2 reshape.64
  37.3 27.8 %all_to_all.19 = bf16[64,2,1024]{2,1,0:T(2,128)(2,1)S(1)} all-to-all(bf16[64,2,1024]{2,1,0:T(2,128)(2,1)S(1)} %reshape.64), channel_id=1, replica_groups=mesh['ep'=64,'fsdp'=4] {'ep'}, dimensions={0} | all-to-all | bytes 524288 | tf_op jit(solution)/shard_map/all_to_all | solution.py:17
  65.1 0.2 reshape.65
  65.3 0.9 copy.21
  66.1 48.2 %all-gather.2.cloned.1.call-done = bf16[2,2048,1024]{2,1,0:T(8,128)(2,1)} async-done(((bf16[2,512,1024]{2,1,0:T(8,128)(2,1)}), bf16[2,2048,1024]{2,1,0:T(8,128)(2,1)}) %all-gather.2.cloned.1.call-update) | async-done | bytes 8388624 | tf_op jit(solution)/shard_map/all_gather | solution.py:38
  114.3 6.0 %fusion = (bf16[1,2048,1024]{2,1,0:T(8,128)(2,1)}, bf16[1,2048,1024]{2,1,0:T(8,128)(2,1)}) fusion(bf16[2,2048,1024]{2,1,0:T(8,128)(2,1)} %all-gather.2.cloned.1.call-done), kind=kLoop, calls=%fused_computation.10 | loop fusion | bytes 16777216 | tf_op jit(solution)/shard_map/split | solution.py:39
  (16 shorter events, 0.2 us)
Async XLA Ops:
  7.2 107.2 %all-gather.2.cloned.1.call-start = ((), (), s32[]{:S(2)}) async-start(), calls=%async_computation.3 | async-start | bytes 10485760 | tf_op jit(solution)/shard_map/all_gather | solution.py:38
  7.9 2.9 %copy-start = (f32[1,512,1024]{2,1,0:T(8,128)S(1)}, f32[1,512,1024]{2,1,0:T(8,128)}, u32[]{:S(2)}) copy-start(f32[1,512,1024]{2,1,0:T(8,128)} %param.10) | copy-start | bytes 6291460
  7.9 3.5 %copy-start.1 = (f32[1,512,1024]{2,1,0:T(8,128)S(1)}, f32[1,512,1024]{2,1,0:T(8,128)}, u32[]{:S(2)}) copy-start(f32[1,512,1024]{2,1,0:T(8,128)} %param.9) | copy-start | bytes 6291460
  20.7 4.0 %copy-start.2 = (f32[1024]{0:T(1024)}, f32[1024]{0:T(1024)S(1)}, u32[]{:S(2)}) copy-start(f32[1024]{0:T(1024)S(1)} %get-tuple-element.7) | copy-start | bytes 12292
  20.7 4.0 %copy-start.3 = (f32[1024]{0:T(1024)}, f32[1024]{0:T(1024)S(1)}, u32[]{:S(2)}) copy-start(f32[1024]{0:T(1024)S(1)} %get-tuple-element.8) | copy-start | bytes 12292
  26.2 0.7 copy-start.4
  26.2 0.7 copy-start.5
Sparse Core Ops, SparseCore 0:
  26.3 87.9 all-gather.1
